TPU v7x, 32 devices: a whole 2x2x4 slice. The times are simulated.
32 devices in a mesh: py: 4 (over y, core), pz: 8 (over z, x).
Axes of the slice: x: 2, y: 2, z: 4, core: 2. Of those that a mesh axis runs over, the one named last changes fastest.
Arguments:
- wavefunctions: float32 [2, 8, 128, 128, 128], P(None, None, 'pz', 'py'), may hold values from -6 to 6
- potential: float32 [128, 128, 128], P('pz', 'py'), may hold values from -4 to 4
- cutoff_sq: int32 [1], replicated, may hold values from 2304 to 4096
- locked_mask: int32 [8], replicated, may hold values 0 or 1
Outputs:
- applied: float32 [2, 8, 128, 128, 128], P(None, None, 'pz', 'py')
- rayleigh: float32 [8], replicated
- residual_norm: float32 [8], replicated
All inputs are finite; a program needn't handle non-finite values.
Results may differ from a plain program's by a relative error of at most 0.00005.
Values sent between devices are 32-bit elements; how exact they have to be, the bound alone decides.
A program may use at most 64 MiB of HBM per device.

v0:
```python
import math
import jax
import jax.numpy as jnp
from jax import lax
from jax.sharding import PartitionSpec as P


def make_tables(length, inverse):
    counter = jnp.arange(length, dtype=jnp.int32)
    phase = counter[:, None] * counter[None, :] % length
    angle = 2.0 * math.pi / length * phase.astype(jnp.float32)
    if inverse:
        return (jnp.cos(angle) / length, jnp.sin(angle) / length)
    return (jnp.cos(angle), -jnp.sin(angle))


def transform_axis(field, axis, tables):
    cosines, sines = tables
    letters = "abcdefgh"[: field.ndim - 1]
    place = axis - 1
    source = letters[:place] + "n" + letters[place + 1 :]
    target = letters[:place] + "k" + letters[place + 1 :]
    form = source + ",kn->" + target
    real_part = field[0]
    imag_part = field[1]
    high = lax.Precision.HIGHEST
    out_real = jnp.einsum(form, real_part, cosines, precision=high) - jnp.einsum(
        form, imag_part, sines, precision=high
    )
    out_imag = jnp.einsum(form, real_part, sines, precision=high) + jnp.einsum(
        form, imag_part, cosines, precision=high
    )
    return jnp.stack([out_real, out_imag])


def signed_square(counter, length):
    signed = jnp.where(counter < length // 2, counter, counter - length)
    return signed * signed


def kinetic_table(first_sq, second_sq, third_sq, cutoff_sq, length):
    total = first_sq[:, None, None] + second_sq[None, :, None] + third_sq[None, None, :]
    keep = (total <= cutoff_sq[0]).astype(jnp.float32)
    return 0.5 * (math.pi / length) ** 2 * total.astype(jnp.float32) * keep


def slab_kinetic(field, cutoff_sq, forward, inverse):
    parts, bands, rows_z, rows_y, length = field.shape
    size_y = lax.axis_size("py")
    size_z = lax.axis_size("pz")
    along_x = transform_axis(field, 4, forward)
    flat = jnp.moveaxis(along_x, 1, 3).reshape(parts, rows_z, rows_y, bands * length)
    planes = lax.all_to_all(
        lax.all_to_all(flat, "py", split_axis=3, concat_axis=2, tiled=True),
        "pz",
        split_axis=3,
        concat_axis=1,
        tiled=True,
    )
    width = planes.shape[3]
    start = lax.axis_index("py") * (bands * length // size_y) + lax.axis_index("pz") * width
    column = start + jnp.arange(width, dtype=jnp.int32)
    full_counter = jnp.arange(length, dtype=jnp.int32)
    full_sq = signed_square(full_counter, length)
    kinetic = kinetic_table(
        full_sq, full_sq, signed_square(column % length, length), cutoff_sq, length
    )
    spectrum = transform_axis(transform_axis(planes, 1, forward), 2, forward) * kinetic
    spatial = transform_axis(transform_axis(spectrum, 2, inverse), 1, inverse)
    returned = lax.all_to_all(
        lax.all_to_all(spatial, "py", split_axis=2, concat_axis=3, tiled=True),
        "pz",
        split_axis=1,
        concat_axis=3,
        tiled=True,
    )
    ordered = returned.reshape(parts, rows_z, rows_y, size_z, size_y, width)
    ordered = jnp.swapaxes(ordered, 3, 4).reshape(parts, rows_z, rows_y, bands, length)
    return transform_axis(jnp.moveaxis(ordered, 3, 1), 4, inverse)


def apply_kinetic(field, cutoff_sq, forward, inverse):
    return slab_kinetic(field, cutoff_sq, forward, inverse)


def body(wavefunctions, potential, cutoff_sq, locked_mask):
    length = wavefunctions.shape[4]
    forward = make_tables(length, False)
    inverse = make_tables(length, True)
    blocks = wavefunctions.shape[1] // 4

    def one_block(block, result):
        piece = lax.dynamic_slice_in_dim(wavefunctions, block * 4, 4, 1)
        done = apply_kinetic(piece, cutoff_sq, forward, inverse)
        return lax.dynamic_update_slice_in_dim(result, done, block * 4, 1)

    kinetic_part = lax.fori_loop(0, blocks, one_block, jnp.zeros_like(wavefunctions))
    applied = kinetic_part + potential[None, None] * wavefunctions
    norm_local = jnp.sum(wavefunctions * wavefunctions, axis=(0, 2, 3, 4))
    correlation_local = jnp.sum(wavefunctions * applied, axis=(0, 2, 3, 4))
    norm_sq, correlation = lax.psum((norm_local, correlation_local), ("py", "pz"))
    rayleigh = correlation / norm_sq
    residual = applied - rayleigh[None, :, None, None, None] * wavefunctions
    residual_sq = lax.psum(jnp.sum(residual * residual, axis=(0, 2, 3, 4)), ("py", "pz"))
    residual_norm = jnp.sqrt(residual_sq / norm_sq) * (1.0 - locked_mask.astype(jnp.float32))
    return (applied, rayleigh, residual_norm)


def solution(mesh):
    in_specs = (P(None, None, "pz", "py", None), P("pz", "py", None), P(), P())
    out_specs = (P(None, None, "pz", "py", None), P(), P())
    return jax.shard_map(body, mesh=mesh, in_specs=in_specs, out_specs=out_specs, check_vma=False)
```

profile of v0, /device:TPU:0, one launch (start us, length us, event | category | flops | bytes accessed | tf_op | source)
XLA Modules:
  0.0 693.6 jit_solution(16688748125790381216)
XLA Ops:
  0.6 2.5 broadcast_in_dim.14
  3.2 599.9 %while.18 = (s32[]{:T(128)}, f32[2,8,16,32,128]{4,3,2,1,0:T(8,128)}, f32[2,8,16,32,128]{4,3,2,1,0:T(8,128)}, s32[1]{0:T(128)}, s32[]{:T(128)}, /*index=5*/s32[]{...) while((s32[]{:T(128)}, ...), condition=%wide.region_1.2_spmd.clone.clone, body=%wide.region_0.1_spmd.clone.clone.sunk | while | flops 9676570624 | bytes 232916592 | solution.py:97
  3.2 2.5 fusion.346
  8.1 2.5 fusion.347
  10.6 2.5 fusion.345
  13.3 7.5 %copy.142 = f32[2,16,32,4,128]{2,1,0,4,3:T(8,128)} copy(f32[2,16,32,4,128]{4,2,1,3,0:T(8,128)S(1)} %maximum_bitcast_fusion.2) | data formatting | bytes 4194304 | tf_op jit(solution)/shard_map/while/body/eval_jaxpr/reshape | solution.py:52
  20.7 6.1 reshape.143
  26.9 30.2 %all_to_all.204 = f32[4,1,131072]{2,1,0:T(1,128)} all-to-all(f32[4,1,131072]{2,1,0:T(1,128)S(1)} %reshape.143), channel_id=1, replica_groups=mesh['py'=4,'pz'=8] {'py'}, dimensions={0} | all-to-all | bytes 4194304 | tf_op jit(solution)/shard_map/while/body/eval_jaxpr/all_to_all | solution.py:54
  57.6 7.7 %reduce.4 = f32[4,131072]{1,0:T(4,128)S(1)} reduce(f32[4,1,131072]{2,1,0:T(1,128)} %all_to_all.204, f32[]{:T(128)} %broadcast.656), dimensions={1}, to_apply=%all_to_all.178.reduce_sub_computation | reduce | bytes 4194308 | tf_op jit(solution)/shard_map/while/body/eval_jaxpr/all_to_all | solution.py:54
  65.3 6.1 reshape.144
  71.4 5.2 copy.143
  78.2 3.1 copy.145
  81.3 6.9 all-to-all-start.1
  89.3 46.3 %all-to-all-done.1 = f32[2,16,128,128]{2,1,0,3:T(8,128)S(1)} async-done(((f32[2,16,128,128]{2,1,0,3:T(8,128)}), f32[2,16,128,128]{2,1,0,3:T(8,128)S(1)}, u32[]{:S(2)}, u32[]{:S(2)}) %all-to-all-start.1) | async-done | bytes 2097184 | tf_op jit(solution)/shard_map/while/body/eval_jaxpr/all_to_all | solution.py:53
  170.9 28.1 %all_to_all.205 = f32[2,128,128,16]{1,3,0,2:T(8,128)S(1)} all-to-all(f32[2,128,128,16]{1,3,0,2:T(8,128)S(1)} %copy.151), channel_id=1, replica_groups=mesh['py'=4,'pz'=8] {'py'}, dimensions={2} | all-to-all | bytes 4194304 | tf_op jit(solution)/shard_map/while/body/eval_jaxpr/all_to_all | solution.py:71
  199.3 4.5 copy.153
  203.8 7.2 %reshape.145 = f32[8,1,65536]{2,1,0:T(1,128)} reshape(f32[128,2,32,64]{3,2,1,0:T(8,128)} %bitcast.327) | data formatting | bytes 4194304 | tf_op jit(solution)/shard_map/while
  211.0 3.9 all-to-all-start.3
  214.9 48.0 %all-to-all-done.3 = f32[8,1,65536]{2,1,0:T(1,128)S(1)} async-done(((f32[8,1,65536]{2,1,0:T(1,128)}), f32[8,1,65536]{2,1,0:T(1,128)S(1)}, u32[]{:S(2)}, u32[]{:S(2)}) %all-to-all-start.3) | async-done | bytes 2097184 | tf_op jit(solution)/shard_map/while/body/eval_jaxpr/all_to_all | solution.py:70
  264.8 7.2 %reduce.5 = f32[8,65536]{1,0:T(8,128)S(1)} reduce(f32[8,1,65536]{2,1,0:T(1,128)} %copy-done, f32[]{:T(128)} %broadcast.657), dimensions={1}, to_apply=%all_to_all.189.reduce_sub_computation | reduce | bytes 4194308 | tf_op jit(solution)/shard_map/while/body/eval_jaxpr/all_to_all | solution.py:70
  272.0 3.6 reshape.146
  275.6 7.0 %copy.154 = f32[2,16,32,8,64]{2,4,3,1,0:T(8,128)} copy(f32[2,16,32,8,64]{4,2,0,1,3:T(8,128)} %bitcast.326) | data formatting | bytes 4194304 | tf_op jit(solution)/shard_map/while/body/eval_jaxpr/all_to_all | solution.py:70
  282.6 7.9 %copy.155 = f32[2,16,32,4,8,16]{2,5,4,3,1,0:T(8,128)} copy(f32[2,16,32,4,8,16]{2,5,3,4,1,0:T(8,128)} %bitcast.320) | data formatting | bytes 4194304 | tf_op jit(solution)/shard_map/while/body/eval_jaxpr/transpose | solution.py:78
  290.5 5.6 copy.156
  308.4 2.5 fusion.347
  313.5 7.5 %copy.142 = f32[2,16,32,4,128]{2,1,0,4,3:T(8,128)} copy(f32[2,16,32,4,128]{4,2,1,3,0:T(8,128)S(1)} %maximum_bitcast_fusion.2) | data formatting | bytes 4194304 | tf_op jit(solution)/shard_map/while/body/eval_jaxpr/reshape | solution.py:52
  321.0 6.1 reshape.143
  327.2 29.1 %all_to_all.204 = f32[4,1,131072]{2,1,0:T(1,128)} all-to-all(f32[4,1,131072]{2,1,0:T(1,128)S(1)} %reshape.143), channel_id=1, replica_groups=mesh['py'=4,'pz'=8] {'py'}, dimensions={0} | all-to-all | bytes 4194304 | tf_op jit(solution)/shard_map/while/body/eval_jaxpr/all_to_all | solution.py:54
  356.8 7.7 %reduce.4 = f32[4,131072]{1,0:T(4,128)S(1)} reduce(f32[4,1,131072]{2,1,0:T(1,128)} %all_to_all.204, f32[]{:T(128)} %broadcast.656), dimensions={1}, to_apply=%all_to_all.178.reduce_sub_computation | reduce | bytes 4194308 | tf_op jit(solution)/shard_map/while/body/eval_jaxpr/all_to_all | solution.py:54
  364.5 6.1 reshape.144
  370.6 5.2 copy.143
  377.5 3.1 copy.145
  380.5 4.0 all-to-all-start.1
  385.6 46.7 %all-to-all-done.1 = f32[2,16,128,128]{2,1,0,3:T(8,128)S(1)} async-done(((f32[2,16,128,128]{2,1,0,3:T(8,128)}), f32[2,16,128,128]{2,1,0,3:T(8,128)S(1)}, u32[]{:S(2)}, u32[]{:S(2)}) %all-to-all-start.1) | async-done | bytes 2097184 | tf_op jit(solution)/shard_map/while/body/eval_jaxpr/all_to_all | solution.py:53
  467.6 28.1 %all_to_all.205 = f32[2,128,128,16]{1,3,0,2:T(8,128)S(1)} all-to-all(f32[2,128,128,16]{1,3,0,2:T(8,128)S(1)} %copy.151), channel_id=1, replica_groups=mesh['py'=4,'pz'=8] {'py'}, dimensions={2} | all-to-all | bytes 4194304 | tf_op jit(solution)/shard_map/while/body/eval_jaxpr/all_to_all | solution.py:71
  496.0 4.5 copy.153
  500.5 7.2 %reshape.145 = f32[8,1,65536]{2,1,0:T(1,128)} reshape(f32[128,2,32,64]{3,2,1,0:T(8,128)} %bitcast.327) | data formatting | bytes 4194304 | tf_op jit(solution)/shard_map/while
  507.7 3.9 all-to-all-start.3
  511.6 48.0 %all-to-all-done.3 = f32[8,1,65536]{2,1,0:T(1,128)S(1)} async-done(((f32[8,1,65536]{2,1,0:T(1,128)}), f32[8,1,65536]{2,1,0:T(1,128)S(1)}, u32[]{:S(2)}, u32[]{:S(2)}) %all-to-all-start.3) | async-done | bytes 2097184 | tf_op jit(solution)/shard_map/while/body/eval_jaxpr/all_to_all | solution.py:70
  561.5 7.2 %reduce.5 = f32[8,65536]{1,0:T(8,128)S(1)} reduce(f32[8,1,65536]{2,1,0:T(1,128)} %copy-done, f32[]{:T(128)} %broadcast.657), dimensions={1}, to_apply=%all_to_all.189.reduce_sub_computation | reduce | bytes 4194308 | tf_op jit(solution)/shard_map/while/body/eval_jaxpr/all_to_all | solution.py:70
  568.7 3.6 reshape.146
  572.3 7.0 %copy.154 = f32[2,16,32,8,64]{2,4,3,1,0:T(8,128)} copy(f32[2,16,32,8,64]{4,2,0,1,3:T(8,128)} %bitcast.326) | data formatting | bytes 4194304 | tf_op jit(solution)/shard_map/while/body/eval_jaxpr/all_to_all | solution.py:70
  579.3 7.9 %copy.155 = f32[2,16,32,4,8,16]{2,5,4,3,1,0:T(8,128)} copy(f32[2,16,32,4,8,16]{2,5,3,4,1,0:T(8,128)} %bitcast.320) | data formatting | bytes 4194304 | tf_op jit(solution)/shard_map/while/body/eval_jaxpr/transpose | solution.py:78
  587.2 5.6 copy.156
  603.1 6.5 multiply_reduce_fusion.1
  609.6 37.5 %all-reduce = (f32[8]{0:T(128)S(1)}, f32[8]{0:T(128)S(1)}) all-reduce(f32[8]{0:T(128)S(1)} %get-tuple-element.349, f32[8]{0:T(128)S(1)} %get-tuple-element.348), channel_id=1, replica_groups=mesh['py'=4,'pz'=8] {'py','pz'}, use_global_device_ids=true, to_apply=%region_3.4 | all-reduce | flops 16 | bytes 128 | tf_op jit(solution)/shard_map/psum | solution.py:101
  647.2 4.2 multiply_reduce_fusion
  651.4 41.5 %psum.23 = f32[8]{0:T(128)S(1)} all-reduce(f32[8]{0:T(128)S(1)} %multiply_reduce_fusion), channel_id=1, replica_groups=mesh['py'=4,'pz'=8] {'py','pz'}, use_global_device_ids=true, to_apply=%region_7.8 | all-reduce | flops 8 | bytes 64 | tf_op jit(solution)/shard_map/psum | solution.py:104
  (106 shorter events, 105.8 us)
Async XLA Ops:
  3.2 599.9 %copy-start.4 = (f32[16,32,128]{2,1,0:T(8,128)S(1)}, f32[16,32,128]{2,1,0:T(8,128)}, u32[]{:S(2)}) copy-start(f32[16,32,128]{2,1,0:T(8,128)} %param.7) | copy-start | bytes 786436
  81.3 54.2 %all-to-all-start.1 = ((f32[2,16,128,128]{2,1,0,3:T(8,128)}), f32[2,16,128,128]{2,1,0,3:T(8,128)S(1)}, u32[]{:S(2)}, u32[]{:S(2)}) async-start(f32[2,16,128,128]{2,1,0,3:T(8,128)} %copy.145), calls=%async_computation.1 | async-start | bytes 4194304 | tf_op jit(solution)/shard_map/while/body/eval_jaxpr/all_to_all | solution.py:53
  138.5 3.5 copy-start.1
  211.0 51.9 %all-to-all-start.3 = ((f32[8,1,65536]{2,1,0:T(1,128)}), f32[8,1,65536]{2,1,0:T(1,128)S(1)}, u32[]{:S(2)}, u32[]{:S(2)}) async-start(f32[8,1,65536]{2,1,0:T(1,128)} %reshape.145), calls=%async_computation.3 | async-start | bytes 4194304 | tf_op jit(solution)/shard_map/while/body/eval_jaxpr/all_to_all | solution.py:70
  262.9 1.4 copy-start
  298.6 2.5 copy-start.2
  301.3 2.0 copy-start.3
  380.5 51.7 %all-to-all-start.1 = ((f32[2,16,128,128]{2,1,0,3:T(8,128)}), f32[2,16,128,128]{2,1,0,3:T(8,128)S(1)}, u32[]{:S(2)}, u32[]{:S(2)}) async-start(f32[2,16,128,128]{2,1,0,3:T(8,128)} %copy.145), calls=%async_computation.1 | async-start | bytes 4194304 | tf_op jit(solution)/shard_map/while/body/eval_jaxpr/all_to_all | solution.py:53
  435.2 3.5 copy-start.1
  507.7 51.9 %all-to-all-start.3 = ((f32[8,1,65536]{2,1,0:T(1,128)}), f32[8,1,65536]{2,1,0:T(1,128)S(1)}, u32[]{:S(2)}, u32[]{:S(2)}) async-start(f32[8,1,65536]{2,1,0:T(1,128)} %reshape.145), calls=%async_computation.3 | async-start | bytes 4194304 | tf_op jit(solution)/shard_map/while/body/eval_jaxpr/all_to_all | solution.py:70
  559.6 1.4 copy-start
  595.2 2.5 copy-start.2
  598.0 2.0 copy-start.3
  647.1 4.2 copy-start.5
  647.2 45.7 %copy-start.6 = (s32[8]{0:T(128)S(1)}, s32[8]{0:T(128)}, u32[]{:S(2)}) copy-start(s32[8]{0:T(128)} %param.9) | copy-start | bytes 100
where the time goes:
time: 697 us; the launch traced here: 694 us
  blocking collectives  195 us (28%)
  waiting for transfers between devices  189 us (27%)
  local copies, waits for them, and re-layouts  156 us (22%)
  matrix products  85.4 us (12%)
  other arithmetic  44.8 us (6%)
  starting transfers between devices  18.7 us (3%)
    all_to_all x2, waiting for transfers between devices, slab_kinetic(): lax.all_to_all(lax.all_to_all(spatial, 'py', split_axis=2, concat_axis=3,...  96 us
    all_to_all x2, waiting for transfers between devices, slab_kinetic(): lax.all_to_all(lax.all_to_all(flat, 'py', split_axis=3, concat_axis=2, ti...  92.9 us
    all_to_all x2, blocking collectives, slab_kinetic(): lax.all_to_all(flat, 'py', split_axis=3, concat_axis=2, tiled=True)  59.3 us
    all_to_all x2, blocking collectives, slab_kinetic(): lax.all_to_all(spatial, 'py', split_axis=2, concat_axis=3, tiled=True)  56.3 us
    while x24, local copies, waits for them, and re-layouts  52.9 us
    psum x1, blocking collectives, body(): lax.psum(jnp.sum(residual * residual, axis=(0, 2, 3, 4)), ('py', 'pz'))  41.5 us
    psum x1, blocking collectives, body(): lax.psum((norm_local, correlation_local), ('py', 'pz'))  37.5 us
    dot_general x12, matrix products, transform_axis(): jnp.einsum(form, imag_part, sines, precision=high)  22.5 us
  transfers between devices with their start and end apart: 4, of which 4 were waited for; matrix products, arithmetic and copies ran while one was open for 0% of the time, Pallas kernels for 0%

commit v1 on v0

--- a/solution.py
+++ b/solution.py
@@ -1,8 +1,33 @@
+import functools
 import math
 import jax
 import jax.numpy as jnp
 from jax import lax
 from jax.sharding import PartitionSpec as P
+from jax.lax import axis_index, axis_size, ppermute
+
+
+def _fill_points(my_data, a_name):
+    y, found_now = (axis_size(a_name), axis_index(a_name))
+    piece_out = my_data.shape[3] // y
+    tile_out = list(my_data.shape)
+    tile_out[3] = piece_out
+    y2 = tile_out[2]
+    tile_out[2] = y2 * y
+    local_now = jnp.zeros(tile_out, my_data.dtype)
+    for src_i in [*range(y)]:
+        raw_out = lax.dynamic_slice_in_dim(
+            my_data, (found_now ^ src_i) * piece_out, piece_out, axis=3
+        )
+        if src_i:
+            raw_out = ppermute(raw_out, a_name, [(dev_j, dev_j ^ src_i) for dev_j in range(y)])
+        local_now = lax.dynamic_update_slice_in_dim(
+            local_now, raw_out, (found_now ^ src_i) * y2, axis=2
+        )
+    return local_now
+
+
+open_ratios = functools.partial(_fill_points, a_name="py")
 
 
 def make_tables(length, inverse):
@@ -50,13 +75,7 @@
     size_z = lax.axis_size("pz")
     along_x = transform_axis(field, 4, forward)
     flat = jnp.moveaxis(along_x, 1, 3).reshape(parts, rows_z, rows_y, bands * length)
-    planes = lax.all_to_all(
-        lax.all_to_all(flat, "py", split_axis=3, concat_axis=2, tiled=True),
-        "pz",
-        split_axis=3,
-        concat_axis=1,
-        tiled=True,
-    )
+    planes = lax.all_to_all(open_ratios(flat), "pz", split_axis=3, concat_axis=1, tiled=True)
     width = planes.shape[3]
     start = lax.axis_index("py") * (bands * length // size_y) + lax.axis_index("pz") * width
     column = start + jnp.arange(width, dtype=jnp.int32)

time: 697 us -> 877 us (1.26)
  local copies, waits for them, and re-layouts: 156 us -> 405 us
  blocking collectives: 195 us -> 136 us
  other arithmetic: 44.8 us -> 29.6 us
    dynamic_update_slice x0 -> x8, local copies, waits for them, and re-layouts: none -> 278 us  [_fill_points(): lax.dynamic_update_slice_in_dim(local_now, raw_out, (found_now ^ src_i) *...]
    all_to_all x2 -> x0, blocking collectives: 59.3 us -> none  [slab_kinetic(): lax.all_to_all(flat, 'py', split_axis=3, concat_axis=2, tiled=True)]
    while x24 -> x28, local copies, waits for them, and re-layouts: 52.9 us -> 31 us
    all_to_all x10 -> x2, local copies, waits for them, and re-layouts: 23.3 us -> 2.43 us  [slab_kinetic(): lax.all_to_all(open_ratios(flat), 'pz', split_axis=3, concat_axis=1, tile...]
    ppermute x0 -> x6, local copies, waits for them, and re-layouts: none -> 19.4 us  [_fill_points(): ppermute(raw_out, a_name, [(dev_j, dev_j ^ src_i) for dev_j in range(y)])]
    all_to_all x2 -> x0, other arithmetic: 15.4 us -> none  [slab_kinetic(): lax.all_to_all(flat, 'py', split_axis=3, concat_axis=2, tiled=True)]
    reshape x2 -> x0, local copies, waits for them, and re-layouts: 15 us -> none  [slab_kinetic(): jnp.moveaxis(along_x, 1, 3).reshape(parts, rows_z, rows_y, bands * length)]
  transfers between devices with their start and end apart: 4 -> 10, of which waited for: 4 -> 4; matrix products, arithmetic and copies ran while one was open for 0% -> 25% of each run, Pallas kernels for 0% -> 0%
where the time goes in v1:
time: 877 us; the launch traced here: 874 us
  local copies, waits for them, and re-layouts  405 us (46%)
  waiting for transfers between devices  190 us (22%)
  blocking collectives  136 us (16%)
  matrix products  85.2 us (10%)
  other arithmetic  29.6 us (3%)
  starting transfers between devices  23.4 us (3%)
    dynamic_update_slice x8, local copies, waits for them, and re-layouts, _fill_points(): lax.dynamic_update_slice_in_dim(local_now, raw_out, (found_now ^ src_i) *...  278 us
    all_to_all x2, waiting for transfers between devices, slab_kinetic(): lax.all_to_all(lax.all_to_all(spatial, 'py', split_axis=2, concat_axis=3,...  96 us
    all_to_all x2, waiting for transfers between devices, slab_kinetic(): lax.all_to_all(open_ratios(flat), 'pz', split_axis=3, concat_axis=1, tile...  94 us
    all_to_all x2, blocking collectives, slab_kinetic(): lax.all_to_all(spatial, 'py', split_axis=2, concat_axis=3, tiled=True)  56.7 us
    psum x1, blocking collectives, body(): lax.psum(jnp.sum(residual * residual, axis=(0, 2, 3, 4)), ('py', 'pz'))  41.5 us
    psum x1, blocking collectives, body(): lax.psum((norm_local, correlation_local), ('py', 'pz'))  37.5 us
    while x28, local copies, waits for them, and re-layouts  31 us
    dot_general x12, matrix products, transform_axis(): jnp.einsum(form, imag_part, sines, precision=high)  22.5 us
  transfers between devices with their start and end apart: 10, of which 4 were waited for; matrix products, arithmetic and copies ran while one was open for 25% of the time, Pallas kernels for 0%

profile of v1, /device:TPU:0, one launch (start us, length us, event | category | flops | bytes accessed | tf_op | source)
XLA Modules:
  0.0 873.9 jit_solution(9117618721708848060)
XLA Ops:
  0.6 2.5 broadcast_in_dim.14
  3.2 780.1 %while.18 = (s32[]{:T(128)}, f32[2,8,16,32,128]{4,3,2,1,0:T(8,128)}, f32[2,8,16,32,128]{4,3,2,1,0:T(8,128)}, s32[1]{0:T(128)}, s32[]{:T(128)}, /*index=5*/s32[]{...) while((s32[]{:T(128)}, ...), condition=%wide.region_1.2_spmd.clone.clone, body=%wide.region_0.1_spmd.clone.clone.sunk | while | flops 9676570624 | bytes 237111504 | solution.py:116
  3.2 2.5 fusion.346
  8.1 2.5 fusion.347
  10.6 2.5 fusion.345
  15.1 2.5 collective-permute-start.1
  21.1 11.5 %dynamic_update_slice.72 = f32[2,16,128,128]{2,1,0,3:T(8,128)} dynamic-update-slice(f32[2,16,128,128]{2,1,0,3:T(8,128)} %broadcast.668, f32[2,16,32,128]{2,1,0,3:T(8,128)S(1)} %copy.149, s32[]{:T(128)} %constant.217.clone.1..sunk, s32[]{:T(128)} %constant.217.clone.1..sunk, s32[]{:T(128)S(6)} %select_n.419, s32[]{:T(128)} %constant.217.clone.1..sunk) | dynamic-update-slice | bytes 1048580 | tf_op jit(solution)/shard_map/while/body/eval_jaxpr/dynamic_update_slice | solution.py:24
  32.6 4.0 copy.150
  36.6 42.5 %dynamic_update_slice.73 = f32[2,16,128,128]{2,1,0,3:T(8,128)S(1)} dynamic-update-slice(f32[2,16,128,128]{2,1,0,3:T(8,128)S(1)} %copy-done.1, f32[2,16,32,128]{2,1,0,3:T(8,128)} %copy.150, s32[]{:T(128)} %constant.217.clone.1..sunk, s32[]{:T(128)} %constant.217.clone.1..sunk, s32[]{:T(128)S(6)} %select_n.420, s32[]{:T(128)} %constant.217.clone.1..sunk) | dynamic-update-slice | bytes 1048580 | tf_op jit(solution)/shard_map/while/body/eval_jaxpr/dynamic_update_slice | solution.py:24
  79.2 3.9 copy.151
  83.0 42.5 %dynamic_update_slice.74 = f32[2,16,128,128]{2,1,0,3:T(8,128)S(1)} dynamic-update-slice(f32[2,16,128,128]{2,1,0,3:T(8,128)S(1)} %dynamic_update_slice.73, f32[2,16,32,128]{2,1,0,3:T(8,128)} %copy.151, s32[]{:T(128)} %constant.217.clone.1..sunk, s32[]{:T(128)} %constant.217.clone.1..sunk, s32[]{:T(128)S(6)} %select_n.421, s32[]{:T(128)} %constant.217.clone.1..sunk) | dynamic-update-slice | bytes 1048580 | tf_op jit(solution)/shard_map/while/body/eval_jaxpr/dynamic_update_slice | solution.py:24
  128.7 42.4 %dynamic_update_slice.75 = f32[2,16,128,128]{2,1,0,3:T(8,128)} dynamic-update-slice(f32[2,16,128,128]{2,1,0,3:T(8,128)} %copy-done.2, f32[2,16,32,128]{2,1,0,3:T(8,128)S(1)} %copy.152, s32[]{:T(128)} %constant.217.clone.1..sunk, s32[]{:T(128)} %constant.217.clone.1..sunk, s32[]{:T(128)S(6)} %select_n.422, s32[]{:T(128)} %constant.217.clone.1..sunk) | dynamic-update-slice | bytes 1048580 | tf_op jit(solution)/shard_map/while/body/eval_jaxpr/dynamic_update_slice | solution.py:24
  171.1 6.6 all-to-all-start
  178.7 46.8 %all-to-all-done = f32[2,16,128,128]{2,1,0,3:T(8,128)S(1)} async-done(((f32[2,16,128,128]{2,1,0,3:T(8,128)}), f32[2,16,128,128]{2,1,0,3:T(8,128)S(1)}, u32[]{:S(2)}, u32[]{:S(2)}) %all-to-all-start) | async-done | bytes 2097184 | tf_op jit(solution)/shard_map/while/body/eval_jaxpr/all_to_all | solution.py:78
  260.8 28.6 %all_to_all.148 = f32[2,128,128,16]{1,3,0,2:T(8,128)S(1)} all-to-all(f32[2,128,128,16]{1,3,0,2:T(8,128)S(1)} %copy.158), channel_id=1, replica_groups=mesh['py'=4,'pz'=8] {'py'}, dimensions={2} | all-to-all | bytes 4194304 | tf_op jit(solution)/shard_map/while/body/eval_jaxpr/all_to_all | solution.py:90
  289.7 4.5 copy.160
  294.2 7.2 reshape.139
  301.4 3.9 all-to-all-start.2
  305.3 48.0 %all-to-all-done.2 = f32[8,1,65536]{2,1,0:T(1,128)S(1)} async-done(((f32[8,1,65536]{2,1,0:T(1,128)}), f32[8,1,65536]{2,1,0:T(1,128)S(1)}, u32[]{:S(2)}, u32[]{:S(2)}) %all-to-all-start.2) | async-done | bytes 2097184 | tf_op jit(solution)/shard_map/while/body/eval_jaxpr/all_to_all | solution.py:89
  355.1 7.2 reduce.2
  362.3 3.6 reshape.140
  365.9 7.0 copy.161
  372.9 7.9 copy.162
  380.8 5.6 copy.163
  398.7 2.5 fusion.347
  401.2 2.5 fusion.345
  410.5 11.4 %dynamic_update_slice.72 = f32[2,16,128,128]{2,1,0,3:T(8,128)} dynamic-update-slice(f32[2,16,128,128]{2,1,0,3:T(8,128)} %broadcast.668, f32[2,16,32,128]{2,1,0,3:T(8,128)S(1)} %copy.149, s32[]{:T(128)} %constant.217.clone.1..sunk, s32[]{:T(128)} %constant.217.clone.1..sunk, s32[]{:T(128)S(6)} %select_n.419, s32[]{:T(128)} %constant.217.clone.1..sunk) | dynamic-update-slice | bytes 1048580 | tf_op jit(solution)/shard_map/while/body/eval_jaxpr/dynamic_update_slice | solution.py:24
  421.9 4.0 copy.150
  425.9 42.5 %dynamic_update_slice.73 = f32[2,16,128,128]{2,1,0,3:T(8,128)S(1)} dynamic-update-slice(f32[2,16,128,128]{2,1,0,3:T(8,128)S(1)} %copy-done.1, f32[2,16,32,128]{2,1,0,3:T(8,128)} %copy.150, s32[]{:T(128)} %constant.217.clone.1..sunk, s32[]{:T(128)} %constant.217.clone.1..sunk, s32[]{:T(128)S(6)} %select_n.420, s32[]{:T(128)} %constant.217.clone.1..sunk) | dynamic-update-slice | bytes 1048580 | tf_op jit(solution)/shard_map/while/body/eval_jaxpr/dynamic_update_slice | solution.py:24
  468.4 3.9 copy.151
  472.3 42.5 %dynamic_update_slice.74 = f32[2,16,128,128]{2,1,0,3:T(8,128)S(1)} dynamic-update-slice(f32[2,16,128,128]{2,1,0,3:T(8,128)S(1)} %dynamic_update_slice.73, f32[2,16,32,128]{2,1,0,3:T(8,128)} %copy.151, s32[]{:T(128)} %constant.217.clone.1..sunk, s32[]{:T(128)} %constant.217.clone.1..sunk, s32[]{:T(128)S(6)} %select_n.421, s32[]{:T(128)} %constant.217.clone.1..sunk) | dynamic-update-slice | bytes 1048580 | tf_op jit(solution)/shard_map/while/body/eval_jaxpr/dynamic_update_slice | solution.py:24
  517.9 42.4 %dynamic_update_slice.75 = f32[2,16,128,128]{2,1,0,3:T(8,128)} dynamic-update-slice(f32[2,16,128,128]{2,1,0,3:T(8,128)} %copy-done.2, f32[2,16,32,128]{2,1,0,3:T(8,128)S(1)} %copy.152, s32[]{:T(128)} %constant.217.clone.1..sunk, s32[]{:T(128)} %constant.217.clone.1..sunk, s32[]{:T(128)S(6)} %select_n.422, s32[]{:T(128)} %constant.217.clone.1..sunk) | dynamic-update-slice | bytes 1048580 | tf_op jit(solution)/shard_map/while/body/eval_jaxpr/dynamic_update_slice | solution.py:24
  560.3 4.0 all-to-all-start
  565.4 47.2 %all-to-all-done = f32[2,16,128,128]{2,1,0,3:T(8,128)S(1)} async-done(((f32[2,16,128,128]{2,1,0,3:T(8,128)}), f32[2,16,128,128]{2,1,0,3:T(8,128)S(1)}, u32[]{:S(2)}, u32[]{:S(2)}) %all-to-all-start) | async-done | bytes 2097184 | tf_op jit(solution)/shard_map/while/body/eval_jaxpr/all_to_all | solution.py:78
  647.9 28.1 %all_to_all.148 = f32[2,128,128,16]{1,3,0,2:T(8,128)S(1)} all-to-all(f32[2,128,128,16]{1,3,0,2:T(8,128)S(1)} %copy.158), channel_id=1, replica_groups=mesh['py'=4,'pz'=8] {'py'}, dimensions={2} | all-to-all | bytes 4194304 | tf_op jit(solution)/shard_map/while/body/eval_jaxpr/all_to_all | solution.py:90
  676.2 4.5 copy.160
  680.7 7.2 reshape.139
  687.9 3.9 all-to-all-start.2
  691.8 48.0 %all-to-all-done.2 = f32[8,1,65536]{2,1,0:T(1,128)S(1)} async-done(((f32[8,1,65536]{2,1,0:T(1,128)}), f32[8,1,65536]{2,1,0:T(1,128)S(1)}, u32[]{:S(2)}, u32[]{:S(2)}) %all-to-all-start.2) | async-done | bytes 2097184 | tf_op jit(solution)/shard_map/while/body/eval_jaxpr/all_to_all | solution.py:89
  741.7 7.2 reduce.2
  748.9 3.6 reshape.140
  752.5 7.0 copy.161
  759.5 7.9 copy.162
  767.4 5.6 copy.163
  783.3 6.5 multiply_reduce_fusion.1
  789.9 37.5 %all-reduce = (f32[8]{0:T(128)S(1)}, f32[8]{0:T(128)S(1)}) all-reduce(f32[8]{0:T(128)S(1)} %get-tuple-element.349, f32[8]{0:T(128)S(1)} %get-tuple-element.348), channel_id=1, replica_groups=mesh['py'=4,'pz'=8] {'py','pz'}, use_global_device_ids=true, to_apply=%region_3.4 | all-reduce | flops 16 | bytes 128 | tf_op jit(solution)/shard_map/psum | solution.py:120
  827.4 4.2 multiply_reduce_fusion
  831.6 41.5 %psum.23 = f32[8]{0:T(128)S(1)} all-reduce(f32[8]{0:T(128)S(1)} %multiply_reduce_fusion), channel_id=1, replica_groups=mesh['py'=4,'pz'=8] {'py','pz'}, use_global_device_ids=true, to_apply=%region_7.8 | all-reduce | flops 8 | bytes 64 | tf_op jit(solution)/shard_map/psum | solution.py:123
  (128 shorter events, 117.2 us)
Async XLA Ops:
  3.2 780.1 %copy-start.6 = (f32[16,32,128]{2,1,0:T(8,128)S(1)}, f32[16,32,128]{2,1,0:T(8,128)}, u32[]{:S(2)}) copy-start(f32[16,32,128]{2,1,0:T(8,128)} %param.7) | copy-start | bytes 786436
  14.6 18.0 %collective-permute-start = (f32[2,16,32,128]{3,2,1,0:T(8,128)}, f32[2,16,32,128]{3,2,1,0:T(8,128)}, u32[]{:S(2)}, u32[]{:S(2)}) collective-permute-start(f32[2,16,32,128]{3,2,1,0:T(8,128)} %get-tuple-element.399), channel_id=1, source_target_pairs={{0,8},{8,0},{16,24},{24,16},{1,9},{9,1},{17,25},{25,17},{2,10},{10... | collective-permute-start | bytes 1572872 | tf_op jit(solution)/shard_map/while/body/eval_jaxpr/ppermute | solution.py:23
  15.1 64.0 %collective-permute-start.1 = (f32[2,16,32,128]{3,2,1,0:T(8,128)}, f32[2,16,32,128]{3,2,1,0:T(8,128)}, u32[]{:S(2)}, u32[]{:S(2)}) collective-permute-start(f32[2,16,32,128]{3,2,1,0:T(8,128)} %get-tuple-element.400), channel_id=1, source_target_pairs={{0,16},{8,24},{16,0},{24,8},{1,17},{9,25},{17,1},{25,9},{2,18},{10... | collective-permute-start | bytes 1572872 | tf_op jit(solution)/shard_map/while/body/eval_jaxpr/ppermute | solution.py:23
  17.6 109.2 %collective-permute-start.2 = (f32[2,16,32,128]{3,2,1,0:T(8,128)}, f32[2,16,32,128]{3,2,1,0:T(8,128)S(1)}, u32[]{:S(2)}, u32[]{:S(2)}) collective-permute-start(f32[2,16,32,128]{3,2,1,0:T(8,128)} %get-tuple-element.401), channel_id=1, source_target_pairs={{0,24},{8,16},{16,8},{24,0},{1,25},{9,17},{17,9},{25,1},{2,26},{10... | collective-permute-start | bytes 1572872 | tf_op jit(solution)/shard_map/while/body/eval_jaxpr/ppermute | solution.py:23
  32.6 4.0 copy-start.1
  125.5 1.3 copy-start.2
  171.1 54.4 %all-to-all-start = ((f32[2,16,128,128]{2,1,0,3:T(8,128)}), f32[2,16,128,128]{2,1,0,3:T(8,128)S(1)}, u32[]{:S(2)}, u32[]{:S(2)}) async-start(f32[2,16,128,128]{2,1,0,3:T(8,128)} %dynamic_update_slice.75), calls=%async_computation | async-start | bytes 4194304 | tf_op jit(solution)/shard_map/while/body/eval_jaxpr/all_to_all | solution.py:78
  228.5 3.4 copy-start.3
  301.4 51.9 %all-to-all-start.2 = ((f32[8,1,65536]{2,1,0:T(1,128)}), f32[8,1,65536]{2,1,0:T(1,128)S(1)}, u32[]{:S(2)}, u32[]{:S(2)}) async-start(f32[8,1,65536]{2,1,0:T(1,128)} %reshape.139), calls=%async_computation.2 | async-start | bytes 4194304 | tf_op jit(solution)/shard_map/while/body/eval_jaxpr/all_to_all | solution.py:89
  353.3 1.3 copy-start
  388.9 2.5 copy-start.4
  391.6 2.0 copy-start.5
  405.2 16.7 %collective-permute-start = (f32[2,16,32,128]{3,2,1,0:T(8,128)}, f32[2,16,32,128]{3,2,1,0:T(8,128)}, u32[]{:S(2)}, u32[]{:S(2)}) collective-permute-start(f32[2,16,32,128]{3,2,1,0:T(8,128)} %get-tuple-element.399), channel_id=1, source_target_pairs={{0,8},{8,0},{16,24},{24,16},{1,9},{9,1},{17,25},{25,17},{2,10},{10... | collective-permute-start | bytes 1572872 | tf_op jit(solution)/shard_map/while/body/eval_jaxpr/ppermute | solution.py:23
  405.2 63.2 %collective-permute-start.1 = (f32[2,16,32,128]{3,2,1,0:T(8,128)}, f32[2,16,32,128]{3,2,1,0:T(8,128)}, u32[]{:S(2)}, u32[]{:S(2)}) collective-permute-start(f32[2,16,32,128]{3,2,1,0:T(8,128)} %get-tuple-element.400), channel_id=1, source_target_pairs={{0,16},{8,24},{16,0},{24,8},{1,17},{9,25},{17,1},{25,9},{2,18},{10... | collective-permute-start | bytes 1572872 | tf_op jit(solution)/shard_map/while/body/eval_jaxpr/ppermute | solution.py:23
  406.1 110.0 %collective-permute-start.2 = (f32[2,16,32,128]{3,2,1,0:T(8,128)}, f32[2,16,32,128]{3,2,1,0:T(8,128)S(1)}, u32[]{:S(2)}, u32[]{:S(2)}) collective-permute-start(f32[2,16,32,128]{3,2,1,0:T(8,128)} %get-tuple-element.401), channel_id=1, source_target_pairs={{0,24},{8,16},{16,8},{24,0},{1,25},{9,17},{17,9},{25,1},{2,26},{10... | collective-permute-start | bytes 1572872 | tf_op jit(solution)/shard_map/while/body/eval_jaxpr/ppermute | solution.py:23
  421.9 4.0 copy-start.1
  514.7 1.3 copy-start.2
  560.3 52.2 %all-to-all-start = ((f32[2,16,128,128]{2,1,0,3:T(8,128)}), f32[2,16,128,128]{2,1,0,3:T(8,128)S(1)}, u32[]{:S(2)}, u32[]{:S(2)}) async-start(f32[2,16,128,128]{2,1,0,3:T(8,128)} %dynamic_update_slice.75), calls=%async_computation | async-start | bytes 4194304 | tf_op jit(solution)/shard_map/while/body/eval_jaxpr/all_to_all | solution.py:78
  615.5 3.4 copy-start.3
  687.9 51.9 %all-to-all-start.2 = ((f32[8,1,65536]{2,1,0:T(1,128)}), f32[8,1,65536]{2,1,0:T(1,128)S(1)}, u32[]{:S(2)}, u32[]{:S(2)}) async-start(f32[8,1,65536]{2,1,0:T(1,128)} %reshape.139), calls=%async_computation.2 | async-start | bytes 4194304 | tf_op jit(solution)/shard_map/while/body/eval_jaxpr/all_to_all | solution.py:89
  739.9 1.3 copy-start
  775.5 2.5 copy-start.4
  778.2 2.0 copy-start.5
  827.4 4.2 copy-start.7
  827.4 45.7 %copy-start.8 = (s32[8]{0:T(128)S(1)}, s32[8]{0:T(128)}, u32[]{:S(2)}) copy-start(s32[8]{0:T(128)} %param.9) | copy-start | bytes 100
